TPU v7x, 32 devices: a whole 2x2x4 slice. The times are simulated.
32 devices in a mesh: vocab: 8 (over z, x), tok: 4 (over y, core).
Axes of the slice: x: 2, y: 2, z: 4, core: 2. Of those that a mesh axis runs over, the one named last changes fastest.
Arguments:
- hidden: bfloat16 [768, 7168], P('tok', 'vocab'), may hold values from -21 to 21
- head_weight: bfloat16 [7168, 8192], P('tok', 'vocab'), may hold values from -0.12695312 to 0.12695312
- targets: int32 [768], P('tok'), may hold values from 0 to 6143
- vocab_mask: int32 [8192], P('vocab'), may hold values from 0 to 1, as said below
- token_grad: float32 [768], P('tok'), may hold values from 16 to 160
Outputs:
- hidden_grad: bfloat16 [768, 7168], P('tok', 'vocab')
- token_loss: float32 [768], P('tok')
Inputs may be any that keep to these rules, and one draw needn't show every extreme that they name: vocab_mask is 1 on the columns below some cut and 0 from it on, with between 1 and 2048 zeros.
All inputs are finite; a program needn't handle non-finite values.
Results may differ from a plain program's by a relative error of at most 0.0051.
Values may be sent and summed in bfloat16 or wider, within the bound.
A program may use at most 64 MiB of HBM per device.

v0:
```python
import jax
import jax.numpy as jnp
from jax import lax
from jax.experimental import pallas as pl
from jax.experimental.pallas import tpu as pltpu
from jax.sharding import PartitionSpec as P


def make_on_device(vocab_size, tok_size):
    share = vocab_size // tok_size
    moves = [
        (b * tok_size + a, (a * share + b % share) * tok_size + b // share)
        for a in range(tok_size)
        for b in range(vocab_size)
    ]
    back = [(there, here) for here, there in moves]

    def on_device(hidden, head_weight, targets, vocab_mask, token_grad):
        rows, feats = hidden.shape
        block_width = head_weight.shape[1]
        moved = lax.ppermute(hidden, ("vocab", "tok"), moves)
        pieces = lax.all_gather(moved, "vocab")
        gathered = (
            pieces.reshape(tok_size, share, rows, feats)
            .transpose(0, 2, 1, 3)
            .reshape(tok_size * rows, share * feats)
        )
        partial_logits = jnp.dot(gathered, head_weight, preferred_element_type=jnp.float32)
        logits = lax.psum_scatter(partial_logits, "tok", scatter_dimension=0, tiled=True)
        first_column = lax.axis_index("vocab") * block_width
        masked = jnp.where(vocab_mask[None, :] == 1, logits, jnp.float32(-1e30))
        local_max = jnp.max(masked, axis=1)
        columns = first_column + jnp.arange(block_width, dtype=jnp.int32)
        onehot = columns[None, :] == targets[:, None]
        local_target = jnp.sum(jnp.where(onehot, logits, jnp.float32(0.0)), axis=1)
        weights = jnp.exp(masked - local_max[:, None])
        local_sum = jnp.sum(weights, axis=1)
        stats = lax.all_gather(jnp.stack([local_max, local_sum, local_target]), "vocab")
        row_max = jnp.max(stats[:, 0], axis=0)
        denominator = jnp.sum(stats[:, 1] * jnp.exp(stats[:, 0] - row_max[None]), axis=0)
        target_logit = jnp.sum(stats[:, 2], axis=0)
        log_norm = row_max + jnp.log(denominator)
        token_loss = log_norm - target_logit
        probabilities = jnp.exp(masked - log_norm[:, None])
        logit_grad = (
            token_grad[:, None] * (probabilities - onehot.astype(jnp.float32))
        ).astype(jnp.bfloat16)
        all_grads = lax.all_gather(logit_grad, "tok", axis=0, tiled=True)
        partial_value = lax.dot_general(
            all_grads,
            head_weight,
            (((1,), (1,)), ((), ())),
            preferred_element_type=jnp.float32,
        )
        blocks = (
            partial_value.reshape(tok_size, rows, share, feats)
            .transpose(0, 2, 1, 3)
            .reshape(vocab_size, rows, feats)
        )
        summed = lax.psum_scatter(blocks, "vocab", scatter_dimension=0, tiled=False)
        hidden_grad = lax.ppermute(summed.astype(jnp.bfloat16), ("vocab", "tok"), back)
        return (hidden_grad, token_loss)

    return on_device


CHUNKS = 3
LATE = (0, 1)
EARLY = (2,)
ORDER = LATE + EARLY
BF = jnp.bfloat16
F32 = jnp.float32


def kernel(
    depth,
    hidden_ref, weight_ref, targets_ref, mask_ref, grad_ref,
    out_ref, loss_ref,
    gath, hb, plog, pair_in, cross_in, cross_out, dl, stats_out, stats_in,
    term_out, term_in, up_in, down_in, up_out, down_out, far_out, far_in, near, mix_out, mix_in,
    load_sem, x_send, x_recv, zu_send, zu_recv, zd_send, zd_recv, t_send, t_recv,
    p_send, p_recv, c_send, c_recv, s_send, s_recv, g_send, g_recv,
    e_send, e_recv, eu_send, eu_recv, ed_send, ed_recv, f_send, f_recv, w_send, w_recv, m_send, m_recv,
):
    rows, feats = hidden_ref.shape
    part = rows // CHUNKS
    width = weight_ref.shape[1]
    me_v = lax.axis_index("vocab")
    me_t = lax.axis_index("tok")
    z, x = me_v // 2, me_v % 2
    y, c = me_t // 2, me_t % 2
    nv = 2 * depth

    def dev(v, t):
        return {"vocab": v, "tok": t}

    def tok_of(r):
        return ((y + r // 2) % 2) * 2 + (c + r % 2) % 2

    other_x = z * 2 + (1 - x)

    def rcopy(src, dst, ss, rs, v, t):
        return pltpu.make_async_remote_copy(
            src_ref=src, dst_ref=dst, send_sem=ss, recv_sem=rs,
            device_id=dev(v, t), device_id_type=pl.DeviceIdType.MESH,
        )

    def span(h):
        return pl.ds(h * part, part)

    loads = [
        pltpu.make_async_copy(hidden_ref.at[span(h)], gath.at[0, z, h], load_sem.at[h])
        for h in range(CHUNKS)
    ]
    for load in loads:
        load.start()

    barrier = pltpu.get_barrier_semaphore()
    for r in range(1, 4):
        pl.semaphore_signal(barrier, inc=1, device_id=dev(me_v, tok_of(r)), device_id_type=pl.DeviceIdType.MESH)
    for k in range(1, nv):
        pl.semaphore_signal(barrier, inc=1, device_id=dev((me_v + k) % nv, me_t), device_id_type=pl.DeviceIdType.MESH)
    pl.semaphore_wait(barrier, 3 + nv - 1)

    top = jnp.concatenate([targets_ref[...].astype(F32), grad_ref[...]], axis=0)
    top = jnp.concatenate([top, jnp.zeros((2, 256 - rows), F32)], axis=1)
    sides = jnp.transpose(jnp.concatenate([top, jnp.zeros((126, 256), F32)], axis=0))[0:rows]
    tok_target = sides[:, 0:1].astype(jnp.int32)
    tok_grad = sides[:, 1:2]

    def x_copy(h):
        return rcopy(gath.at[0, z, h], gath.at[1, z, h], x_send.at[h], x_recv.at[h], other_x, me_t)

    def up_copy(q, zz, h):
        return rcopy(gath.at[q, zz, h], gath.at[q, zz, h], zu_send.at[q, zz, h], zu_recv.at[q, zz, h], me_v + 2, me_t)

    def down_copy(q, zz, h):
        return rcopy(gath.at[q, zz, h], gath.at[q, zz, h], zd_send.at[q, zz, h], zd_recv.at[q, zz, h], me_v - 2, me_t)

    def rel(zz):
        return 2 * ((zz // 2 + y) % 2) + (zz % 2 + c) % 2

    def t_copy(q, zz, h):
        r = rel(zz)
        return rcopy(gath.at[q, zz, h], hb.at[q, r, h], t_send.at[q, zz, h], t_recv.at[q, r, h], me_v, zz)

    def pass_on(q, zz, h):
        @pl.when(zz != me_t)
        def _():
            t_copy(q, zz, h).start()

    def late_x(r, h):
        source = gath.at[0, me_t, h] if r == 0 else hb.at[0, r, h]
        return rcopy(source, hb.at[1, r, h], w_send.at[r, h], w_recv.at[r, h], other_x, me_t)

    def await_own(r, h):
        rcopy(gath.at[0, 0, h], hb.at[0, r, h], t_send.at[0, 0, h], t_recv.at[0, r, h], me_v, tok_of(1)).wait_recv()

    def late_others():
        for h in LATE:
            for r in range(1, 4):
                await_own(r, h)
                late_x(r, h).start()

    distance = jnp.where(z > me_t, z - me_t, me_t - z)
    for h in range(CHUNKS):
        loads[h].wait()
    for h in EARLY:
        x_copy(h).start()
    for s in range(depth):
        for h in ORDER:
            if h == EARLY[0]:
                @pl.when(distance == s)
                def _():
                    for late in LATE:
                        late_x(0, late).start()

                if s > 0:
                    @pl.when(distance == s - 1)
                    def _():
                        late_others()

                if s == depth - 1:
                    @pl.when(distance == s)
                    def _():
                        late_others()

            for q in range(1 if h in LATE else 2):
                if s == 0:
                    if q == 1:
                        x_copy(h).wait_recv()

                    @pl.when(z < depth - 1)
                    def _():
                        up_copy(q, z, h).start()

                    @pl.when(z > 0)
                    def _():
                        down_copy(q, z, h).start()

                    pass_on(q, z, h)
                else:
                    @pl.when(z - s >= 0)
                    def _():
                        up_copy(q, z - s, h).wait_recv()

                        @pl.when(z < depth - 1)
                        def _():
                            up_copy(q, z - s, h).start()

                        pass_on(q, z - s, h)

                    @pl.when(z + s < depth)
                    def _():
                        down_copy(q, z + s, h).wait_recv()

                        @pl.when(z > 0)
                        def _():
                            down_copy(q, z + s, h).start()

                        pass_on(q, z + s, h)

    for h in range(CHUNKS):
        hb[0, 0, h] = gath[0, me_t, h]
    for h in EARLY:
        hb[1, 0, h] = gath[1, me_t, h]

    def weight_rows(q):
        owner = (x + q) % 2
        return pl.ds(pl.multiple_of(owner * feats, 128), feats)

    tile = 256

    def logits_of(r0, nr, group):
        c0, nc = len(LATE) * group, len((LATE, EARLY)[group])

        @pl.loop(0, width // tile)
        def _(j):
            cols = pl.ds(pl.multiple_of(j * tile, tile), tile)
            total = None
            for q in range(2):
                lhs = hb[q, pl.ds(r0, nr), pl.ds(c0, nc)].reshape(nr * nc * part, feats)
                term = jnp.dot(lhs, weight_ref[weight_rows(q), cols], preferred_element_type=F32)
                total = term if total is None else total + term
            plog[pl.ds(r0, nr), pl.ds(c0 * part, nc * part), cols] = total.reshape(nr, nc * part, tile)

    def group_rows(group):
        return pl.ds(part * len(LATE) * group, part * len((LATE, EARLY)[group]))

    def pair_copy(k, group):
        return rcopy(
            plog.at[1 + 2 * k, group_rows(group)], pair_in.at[k, group_rows(group)],
            p_send.at[k, group], p_recv.at[k, group], me_v, tok_of(1),
        )

    def cross_copy(group):
        return rcopy(
            cross_out.at[group_rows(group)], cross_in.at[group_rows(group)],
            c_send.at[group], c_recv.at[group], me_v, tok_of(2),
        )

    def cross_over(group):
        pair_copy(1, group).wait_recv()
        cross_out[group_rows(group), :] = plog[2, group_rows(group), :] + pair_in[1, group_rows(group), :]
        cross_copy(group).start()

    for r in range(1, 4):
        for h in EARLY:
            for q in range(2):
                rcopy(gath.at[q, 0, h], hb.at[q, r, h], t_send.at[q, 0, h], t_recv.at[q, r, h], me_v, tok_of(1)).wait_recv()
    logits_of(0, 4, 1)
    pair_copy(1, 1).start()
    pair_copy(0, 1).start()
    cross_over(1)
    for r in (2, 3):
        for h in LATE:
            late_x(r, h).wait_recv()
    logits_of(2, 2, 0)
    pair_copy(1, 0).start()
    cross_over(0)
    for r in (0, 1):
        for h in LATE:
            late_x(r, h).wait_recv()
    logits_of(0, 2, 0)
    pair_copy(0, 0).start()
    for group in (1, 0):
        pair_copy(0, group).wait_recv()
    plog[0] = plog[0] + pair_in[0]
    for group in (1, 0):
        cross_copy(group).wait_recv()
    logits = plog[0] + cross_in[...]

    masked = jnp.where(mask_ref[...] == 1, logits, jnp.float32(-1e30))
    local_max = jnp.max(masked, axis=1, keepdims=True)
    columns = me_v * width + lax.broadcasted_iota(jnp.int32, (rows, width), 1)
    onehot = columns == tok_target
    local_target = jnp.sum(jnp.where(onehot, logits, 0.0), axis=1, keepdims=True)
    local_sum = jnp.sum(jnp.exp(masked - local_max), axis=1, keepdims=True)
    lanes = lax.broadcasted_iota(jnp.int32, (rows, 128), 1)
    packed = jnp.where(lanes == 0, local_max, jnp.where(lanes == 1, local_sum, local_target))
    tall = jnp.concatenate([packed, jnp.zeros((256 - rows, 128), F32)], axis=0)
    mine = jnp.transpose(tall)[0:8]
    stats_out[...] = mine
    stats_in[me_v] = mine
    plog[0] = masked

    def stat_copy(k):
        return rcopy(stats_out, stats_in.at[me_v], s_send.at[k], s_recv.at[me_v], (me_v + k) % nv, me_t)

    for k in range(1, nv):
        stat_copy(k).start()
    for k in range(1, nv):
        source = (me_v + nv - k) % nv
        rcopy(stats_out, stats_in.at[source], s_send.at[k], s_recv.at[source], source, me_t).wait_recv()
    row_max = stats_in[0][0:1]
    for v in range(1, nv):
        row_max = jnp.maximum(row_max, stats_in[v][0:1])
    denominator = jnp.zeros_like(row_max)
    target_logit = jnp.zeros_like(row_max)
    for v in range(nv):
        got = stats_in[v]
        denominator += got[1:2] * jnp.exp(got[0:1] - row_max)
        target_logit += got[2:3]
    log_norm = row_max + jnp.log(denominator)
    loss_ref[...] = (log_norm - target_logit)[:, 0:rows]
    column = jnp.transpose(jnp.broadcast_to(log_norm, (128, 256)))[0:rows, 0:1]
    probabilities = jnp.exp(plog[0] - column)
    dl[0] = (tok_grad * (probabilities - onehot.astype(F32))).astype(BF)

    def grad_copy(i):
        if i == 0:
            return rcopy(dl.at[0], dl.at[2], g_send.at[0], g_recv.at[0], me_v, tok_of(2))
        if i == 1:
            return rcopy(dl.at[0], dl.at[1], g_send.at[1], g_recv.at[1], me_v, tok_of(1))
        return rcopy(dl.at[2], dl.at[3], g_send.at[2], g_recv.at[2], me_v, tok_of(1))

    grad_copy(0).start()
    grad_copy(1).start()

    def term_copy(q, r, h):
        return rcopy(
            term_out.at[q, r, h], term_in.at[q, me_t, h], e_send.at[q, r, h], e_recv.at[q, r, h], me_v, tok_of(r)
        )

    def mix_copy(r, h):
        return rcopy(mix_out.at[r, h], mix_in.at[r, h], m_send.at[r, h], m_recv.at[r, h], other_x, me_t)

    def terms_of(q, r0, nr):
        lhs = dl[pl.ds(r0, nr)].reshape(nr * rows, width)
        value = lax.dot_general(
            lhs, weight_ref[weight_rows(q), :], (((1,), (1,)), ((), ())), preferred_element_type=F32
        ).reshape(nr, CHUNKS, part, feats)
        for i in range(nr):
            r = r0 + i
            for h in EARLY:
                if r == 0:
                    term_in[q, me_t, h] = value[i, h].astype(BF)
                else:
                    term_out[q, r, h] = value[i, h].astype(BF)
                    term_copy(q, r, h).start()
            for h in LATE:
                if q == 0:
                    near[r, h] = value[i, h]
                else:
                    mix_out[r, h] = value[i, h].astype(BF)
                    mix_copy(r, h).start()

    grad_copy(1).wait_recv()
    for q in (1, 0):
        terms_of(q, 0, 2)
    grad_copy(0).wait_recv()
    grad_copy(2).start()
    for q in (1, 0):
        terms_of(q, 2, 1)
    grad_copy(2).wait_recv()
    for q in (1, 0):
        terms_of(q, 3, 1)
    for r in range(4):
        for h in LATE:
            mix_copy(r, h).wait_recv()
            both = (near[r, h] + mix_in[r, h].astype(F32)).astype(BF)
            if r == 0:
                term_in[0, me_t, h] = both
            else:
                term_out[0, r, h] = both
                term_copy(0, r, h).start()

    def eu_copy(q, zz, h):
        return rcopy(up_out.at[q, zz, h], up_in.at[q, zz, h], eu_send.at[q, zz, h], eu_recv.at[q, zz, h], me_v + 2, me_t)

    def ed_copy(q, zz, h):
        return rcopy(down_out.at[q, zz, h], down_in.at[q, zz, h], ed_send.at[q, zz, h], ed_recv.at[q, zz, h], me_v - 2, me_t)

    def far_copy(h):
        return rcopy(far_out.at[h], far_in.at[h], f_send.at[h], f_recv.at[h], other_x, me_t)

    streams = [(q, h) for h in EARLY for q in (1, 0)] + [(0, h) for h in LATE]
    for q, h in streams:
        if True:
            for r in (1, 2, 3):
                rcopy(term_out.at[q, r, h], term_in.at[q, tok_of(r), h], e_send.at[q, r, h], e_recv.at[q, r, h], me_v, tok_of(r)).wait_recv()
            for k in range(depth - 1, 0, -1):
                @pl.when(z + k < depth)
                def _():
                    zz = z + k

                    @pl.when(z > 0)
                    def _():
                        eu_copy(q, zz, h).wait_recv()
                        up_out[q, zz, h] = (
                            term_in[q, zz, h].astype(F32) + up_in[q, zz, h].astype(F32)
                        ).astype(BF)

                    @pl.when(z == 0)
                    def _():
                        up_out[q, zz, h] = term_in[q, zz, h]

                    eu_copy(q, zz, h).start()

                @pl.when(z - k >= 0)
                def _():
                    zz = z - k

                    @pl.when(z < depth - 1)
                    def _():
                        ed_copy(q, zz, h).wait_recv()
                        down_out[q, zz, h] = (
                            term_in[q, zz, h].astype(F32) + down_in[q, zz, h].astype(F32)
                        ).astype(BF)

                    @pl.when(z == depth - 1)
                    def _():
                        down_out[q, zz, h] = term_in[q, zz, h]

                    ed_copy(q, zz, h).start()

    for q, h in streams:
        if True:
            @pl.when(z > 0)
            def _():
                eu_copy(q, z, h).wait_recv()

            @pl.when(z < depth - 1)
            def _():
                ed_copy(q, z, h).wait_recv()

            def total():
                own = term_in[q, z, h].astype(F32)
                below = jnp.where(z > 0, up_in[q, z, h].astype(F32), 0.0)
                above = jnp.where(z < depth - 1, down_in[q, z, h].astype(F32), 0.0)
                return own + below + above

            if q == 1:
                far_out[h] = total().astype(BF)
                far_copy(h).start()
            elif h in LATE:
                out_ref[span(h), :] = total().astype(BF)
            else:
                far_copy(h).wait_recv()
                out_ref[span(h), :] = (total() + far_in[h].astype(F32)).astype(BF)

    for h in range(CHUNKS):
        if h in EARLY:
            x_copy(h).wait_send()
            far_copy(h).wait_send()
        else:
            for r in range(4):
                late_x(r, h).wait_send()
                mix_copy(r, h).wait_send()
        for q in range(1 if h in LATE else 2):
            for s in range(depth):
                @pl.when(z - s >= 0)
                def _():
                    @pl.when(z < depth - 1)
                    def _():
                        up_copy(q, z - s, h).wait_send()

                @pl.when(z + s < depth)
                def _():
                    @pl.when(z > 0)
                    def _():
                        down_copy(q, z + s, h).wait_send()

                @pl.when(me_t != s)
                def _():
                    t_copy(q, s, h).wait_send()

            for k in range(1, depth):
                @pl.when(z + k < depth)
                def _():
                    eu_copy(q, z + k, h).wait_send()

                @pl.when(z - k >= 0)
                def _():
                    ed_copy(q, z - k, h).wait_send()

            for r in range(1, 4):
                term_copy(q, r, h).wait_send()
    for group in range(2):
        for k in range(2):
            pair_copy(k, group).wait_send()
        cross_copy(group).wait_send()
    for k in range(1, nv):
        stat_copy(k).wait_send()
    for i in range(3):
        grad_copy(i).wait_send()


def fused(vocab_size, tok_size):
    depth = vocab_size // 2

    def on_device(hidden, head_weight, targets, vocab_mask, token_grad):
        rows, feats = hidden.shape
        width = head_weight.shape[1]
        part = rows // CHUNKS
        dma = pltpu.SemaphoreType.DMA
        block = (CHUNKS, part, feats)
        by_q = (2, depth, CHUNKS)
        vmem = pl.BlockSpec(memory_space=pltpu.VMEM)
        hidden_grad, loss = pl.pallas_call(
            lambda *refs: kernel(depth, *refs),
            out_shape=(
                jax.ShapeDtypeStruct((rows, feats), BF),
                jax.ShapeDtypeStruct((1, rows), F32),
            ),
            in_specs=[pl.BlockSpec(memory_space=pltpu.HBM)] + [vmem] * 4,
            out_specs=(vmem, vmem),
            scratch_shapes=[
                pltpu.VMEM((2, depth) + block, BF),
                pltpu.VMEM((2, 4) + block, BF),
                pltpu.VMEM((4, rows, width), F32),
                pltpu.VMEM((2, rows, width), F32),
                pltpu.VMEM((rows, width), F32),
                pltpu.VMEM((rows, width), F32),
                pltpu.VMEM((4, rows, width), BF),
                pltpu.VMEM((8, 256), F32),
                pltpu.VMEM((vocab_size, 8, 256), F32),
                pltpu.VMEM((2, 4) + block, BF),
                pltpu.VMEM((2, 4) + block, BF),
                pltpu.VMEM((2, depth) + block, BF),
                pltpu.VMEM((2, depth) + block, BF),
                pltpu.VMEM((2, depth) + block, BF),
                pltpu.VMEM((2, depth) + block, BF),
                pltpu.VMEM(block, BF),
                pltpu.VMEM(block, BF),
                pltpu.VMEM((4,) + block, F32),
                pltpu.VMEM((4,) + block, BF),
                pltpu.VMEM((4,) + block, BF),
                dma((CHUNKS,)), dma((CHUNKS,)), dma((CHUNKS,)),
                dma(by_q), dma(by_q), dma(by_q), dma(by_q), dma(by_q), dma(by_q),
                dma((2, 2)), dma((2, 2)), dma((2,)), dma((2,)),
                dma((vocab_size,)), dma((vocab_size,)), dma((3,)), dma((3,)),
                dma(by_q), dma(by_q), dma(by_q), dma(by_q), dma(by_q), dma(by_q),
                dma((CHUNKS,)), dma((CHUNKS,)),
                dma((4, CHUNKS)), dma((4, CHUNKS)), dma((4, CHUNKS)), dma((4, CHUNKS)),
            ],
            compiler_params=pltpu.CompilerParams(
                collective_id=0, has_side_effects=True, vmem_limit_bytes=60 * 1024 * 1024
            ),
        )(hidden, head_weight, targets[None, :], vocab_mask[None, :], token_grad[None, :])
        return (hidden_grad, loss.reshape(rows))

    return on_device


def solution(mesh):
    placed = (P("tok", "vocab"), P("tok", "vocab"), P("tok"), P("vocab"), P("tok"))
    vocab_size, tok_size = mesh.shape["vocab"], mesh.shape["tok"]

    def body(hidden, *rest):
        fits = tok_size == 4 and vocab_size == 2 * tok_size and hidden.shape[1] % 128 == 0
        build = fused if fits and hidden.shape[0] <= 256 else make_on_device
        return build(vocab_size, tok_size)(hidden, *rest)

    return jax.shard_map(
        body,
        mesh=mesh,
        in_specs=placed,
        out_specs=(P("tok", "vocab"), P("tok")),
        check_vma=False,
    )
```

profile of v0, /device:TPU:0, one launch (start us, length us, event | category | flops | bytes accessed | tf_op | source)
XLA Modules:
  0.0 140.3 jit_solution(2310617605267895350)
XLA Ops:
  0.6 136.7 %shard_map.68 = (bf16[192,896]{1,0:T(8,128)(2,1)}, f32[1,192]{1,0:T(1,128)}) custom-call(bf16[192,896]{1,0:T(8,128)(2,1)} %refs_0_.1, bf16[1792,1024]{1,0:T(8,128)(2,1)} %refs_1_.1, s32[1,192]{1,0:T(1,128)} %bitcast.5, s32[1,1024]{1,0:T(1,128)} %bitcast.4, f32[1,192]{1,0:T(1,128)} %bitcast.6), custom_call_target="tpu_custom_call" | custom-call | tf_op jit(solution)/shard_map/pallas_call | solution.py:520
  137.4 1.7 %copy.9 = bf16[192,896]{1,0:T(8,128)(2,1)} copy(bf16[192,896]{1,0:T(8,128)(2,1)} %get-tuple-element.8) | data formatting | bytes 688128
  139.1 1.2 copy.10
where the time goes:
time: 140 us
  Pallas kernels  137 us (98%)
  local copies, waits for them, and re-layouts  2.93 us (2%)
    pallas_call x1, Pallas kernels, on_device(): pl.pallas_call(lambda *refs: kernel(depth, *refs), out_shape=(jax.ShapeDt...  137 us
    unnamed x2, local copies, waits for them, and re-layouts  2.93 us

commit v1 on v0

v1 whole, which is shorter than its diff:
```python
import jax
import jax.numpy as jnp
from jax import lax
from jax.experimental import pallas as pl
from jax.experimental.pallas import tpu as pltpu
from jax.sharding import PartitionSpec as P


def make_on_device(vocab_size, tok_size):
    share = vocab_size // tok_size
    moves = [
        (b * tok_size + a, (a * share + b % share) * tok_size + b // share)
        for a in range(tok_size)
        for b in range(vocab_size)
    ]
    back = [(there, here) for here, there in moves]

    def on_device(hidden, head_weight, targets, vocab_mask, token_grad):
        rows, feats = hidden.shape
        block_width = head_weight.shape[1]
        moved = lax.ppermute(hidden, ("vocab", "tok"), moves)
        pieces = lax.all_gather(moved, "vocab")
        gathered = (
            pieces.reshape(tok_size, share, rows, feats)
            .transpose(0, 2, 1, 3)
            .reshape(tok_size * rows, share * feats)
        )
        partial_logits = jnp.dot(gathered, head_weight, preferred_element_type=jnp.float32)
        logits = lax.psum_scatter(partial_logits, "tok", scatter_dimension=0, tiled=True)
        first_column = lax.axis_index("vocab") * block_width
        masked = jnp.where(vocab_mask[None, :] == 1, logits, jnp.float32(-1e30))
        local_max = jnp.max(masked, axis=1)
        columns = first_column + jnp.arange(block_width, dtype=jnp.int32)
        onehot = columns[None, :] == targets[:, None]
        local_target = jnp.sum(jnp.where(onehot, logits, jnp.float32(0.0)), axis=1)
        weights = jnp.exp(masked - local_max[:, None])
        local_sum = jnp.sum(weights, axis=1)
        stats = lax.all_gather(jnp.stack([local_max, local_sum, local_target]), "vocab")
        row_max = jnp.max(stats[:, 0], axis=0)
        denominator = jnp.sum(stats[:, 1] * jnp.exp(stats[:, 0] - row_max[None]), axis=0)
        target_logit = jnp.sum(stats[:, 2], axis=0)
        log_norm = row_max + jnp.log(denominator)
        token_loss = log_norm - target_logit
        probabilities = jnp.exp(masked - log_norm[:, None])
        logit_grad = (
            token_grad[:, None] * (probabilities - onehot.astype(jnp.float32))
        ).astype(jnp.bfloat16)
        all_grads = lax.all_gather(logit_grad, "tok", axis=0, tiled=True)
        partial_value = lax.dot_general(
            all_grads,
            head_weight,
            (((1,), (1,)), ((), ())),
            preferred_element_type=jnp.float32,
        )
        blocks = (
            partial_value.reshape(tok_size, rows, share, feats)
            .transpose(0, 2, 1, 3)
            .reshape(vocab_size, rows, feats)
        )
        summed = lax.psum_scatter(blocks, "vocab", scatter_dimension=0, tiled=False)
        hidden_grad = lax.ppermute(summed.astype(jnp.bfloat16), ("vocab", "tok"), back)
        return (hidden_grad, token_loss)

    return on_device


GROUPS = 3
EXTRA = 128
BF = jnp.bfloat16
F32 = jnp.float32
I16 = jnp.int16


def schedule(groups):
    period, base = 29.5 / groups, 11.0
    took = {1: 0.0, 2: 3.0, 3: 3.0, 4: 3.0 + 8.4 / groups, 5: 4.7, 6: 2.2 + 8.4 / groups, 7: 1.3, 8: 4.5, 9: 4.5, 10: 4.5}
    events = []
    for g in range(groups):
        at = base + period * (g + 1)
        for step in range(1, 11):
            at += took[step]
            events.append((at, step, g))
    return [(step, g) for _, step, g in sorted(events)]


def kernel(
    groups,
    hidden_ref, weight_ref, targets_ref, mask_ref, grad_ref,
    out_ref, loss_ref,
    hid, wbuf, hb, plog, pin, xo, xi, msk, stats_out, stats_in, loss_rows, dl,
    mix_out, mix_in, near, eo, tin, fin,
    l_sem, w_sem, a_send, a_recv, x_send, x_recv, p_send, p_recv, c_send, c_recv,
    s_send, s_recv, d_send, d_recv, m_send, m_recv, e_send, f_recv, t_recv, r_send,
):
    rows, feats = hidden_ref.shape
    m = rows // groups
    width = weight_ref.shape[1]
    me_v = lax.axis_index("vocab")
    me_t = lax.axis_index("tok")
    z, x = me_v // 2, me_v % 2
    y, c = me_t // 2, me_t % 2
    nv = 8

    def dev(v, t):
        return {"vocab": v, "tok": t}

    def tok_of(r):
        return ((y + r // 2) % 2) * 2 + (c + r % 2) % 2

    other_x = z * 2 + (1 - x)

    def rcopy(src, dst, ss, rs, v, t):
        return pltpu.make_async_remote_copy(
            src_ref=src, dst_ref=dst, send_sem=ss, recv_sem=rs,
            device_id=dev(v, t), device_id_type=pl.DeviceIdType.MESH,
        )

    loads = [pltpu.make_async_copy(hidden_ref.at[pl.ds(g * m, m)], hid.at[g], l_sem.at[g]) for g in range(groups)]
    for load in loads:
        load.start()
    weights = pltpu.make_async_copy(weight_ref, wbuf, w_sem)
    weights.start()

    barrier = pltpu.get_barrier_semaphore()
    for k in range(4):
        for r in range(4):
            if k or r:
                pl.semaphore_signal(
                    barrier, inc=1, device_id=dev(((z + k) % 4) * 2 + x, tok_of(r)), device_id_type=pl.DeviceIdType.MESH
                )
        pl.semaphore_signal(
            barrier, inc=1, device_id=dev(((z + k) % 4) * 2 + 1 - x, me_t), device_id_type=pl.DeviceIdType.MESH
        )
    pl.semaphore_wait(barrier, 19)

    home = me_t == z

    def a_copy(g, zz):
        return rcopy(hid.at[g], hb.at[0, g, me_t], a_send.at[g, zz], a_recv.at[g, me_t], zz * 2 + x, z)

    def x_copy(g, t):
        return rcopy(hb.at[0, g, t], hb.at[1, g, t], x_send.at[g, t], x_recv.at[g, t], other_x, me_t)

    def x_own(g):
        return rcopy(hid.at[g], hb.at[1, g, me_t], x_send.at[g, me_t], x_recv.at[g, me_t], other_x, me_t)

    for g in range(groups):
        loads[g].wait()
        for k in (3, 2, 1):
            @pl.when(z + k < 4)
            def _():
                a_copy(g, z + k).start()

            @pl.when(z - k >= 0)
            def _():
                a_copy(g, z - k).start()

        @pl.when(jnp.logical_not(home))
        def _():
            a_copy(g, z).start()

        @pl.when(home)
        def _():
            x_own(g).start()

    @pl.when(home)
    def _():
        for g in range(groups):
            hb[0, g, me_t] = hid[g]

    top = jnp.concatenate([targets_ref[...].astype(F32), grad_ref[...]], axis=0)
    top = jnp.concatenate([top, jnp.zeros((2, 256 - rows), F32)], axis=1)
    sides = jnp.transpose(jnp.concatenate([top, jnp.zeros((126, 256), F32)], axis=0))
    columns = me_v * width + lax.broadcasted_iota(jnp.int32, (m, width), 1)

    def onehot_of(g):
        return columns == sides[g * m:(g + 1) * m, 0:1].astype(jnp.int32)

    def weight_rows(q):
        owner = (x + q) % 2
        return pl.ds(pl.multiple_of(owner * feats, 128), feats)

    def pair_copy(g, k):
        return rcopy(plog.at[g, tok_of(1 + 2 * k)], pin.at[g, k], p_send.at[g, k], p_recv.at[g, k], me_v, tok_of(1))

    def cross_copy(g):
        return rcopy(xo.at[g], xi.at[g], c_send.at[g], c_recv.at[g], me_v, tok_of(2))

    def stat_copy(g, k):
        return rcopy(stats_out.at[g], stats_in.at[g, me_v], s_send.at[g, k], s_recv.at[g, me_v], (me_v + k) % nv, me_t)

    def grad_copy(g, i):
        t = tok_of(2) if i == 2 else me_t
        return rcopy(dl.at[g, t], dl.at[g, t], d_send.at[g, i], d_recv.at[g, i], me_v, tok_of(2 if i == 0 else 1))

    def mix_copy(g, t):
        return rcopy(mix_out.at[g, t], mix_in.at[g, t], m_send.at[g, t], m_recv.at[g, t], other_x, me_t)

    def pass_copy(g, t):
        return rcopy(eo.at[g, t], tin.at[g, c], e_send.at[g, t], t_recv.at[g, c], me_v, t)

    def near_copy(g, t):
        return rcopy(eo.at[g, t], fin.at[g, z], e_send.at[g, t], f_recv.at[g, z], me_v, t)

    def far_copy(g, t):
        return rcopy(eo.at[g, t], fin.at[g, z], e_send.at[g, t], f_recv.at[g, z], me_t * 2 + x, t)

    def relay_copy(g, cc):
        return rcopy(tin.at[g, cc], fin.at[g, z], r_send.at[g, cc], f_recv.at[g, z], ((1 - y) * 2 + cc) * 2 + x, me_t)

    tile = 256

    def spread(g):
        for t in range(4):
            @pl.when(jnp.logical_not(home & (me_t == t)))
            def _():
                a_copy_in = rcopy(hid.at[g], hb.at[0, g, t], a_send.at[g, 0], a_recv.at[g, t], me_v, t)
                a_copy_in.wait_recv()
                x_copy(g, t).start()

    def logits_of(g):
        if g == 0:
            weights.wait()
        for t in range(4):
            x_copy(g, t).wait_recv()

        @pl.loop(0, width // tile)
        def _(j):
            cols = pl.ds(pl.multiple_of(j * tile, tile), tile)
            total = None
            for q in range(2):
                lhs = hb[q, g].reshape(4 * m, feats)
                term = jnp.dot(lhs, wbuf[weight_rows(q), cols], preferred_element_type=F32)
                total = term if total is None else total + term
            plog[g, :, :, cols] = total.reshape(4, m, tile)

        pair_copy(g, 1).start()
        pair_copy(g, 0).start()

    def cross_over(g):
        pair_copy(g, 1).wait_recv()
        value = plog[g, tok_of(2)] + pin[g, 1]
        top_of = jnp.max(jnp.abs(value), axis=1, keepdims=True)
        power = jnp.ceil(jnp.log2(jnp.maximum(top_of, jnp.float32(1e-20))) + jnp.float32(0.001))
        coded = jnp.round(value * jnp.exp2(15.0 - power)).astype(jnp.int32)
        xo[g, :, 0:width] = coded.astype(I16)
        xo[g, :, width:width + EXTRA] = jnp.broadcast_to(power.astype(jnp.int32), (m, EXTRA)).astype(I16)
        cross_copy(g).start()

    def softmax_of(g):
        pair_copy(g, 0).wait_recv()
        near_half = plog[g, me_t] + pin[g, 0]
        cross_copy(g).wait_recv()
        power = xi[g, :, width:width + EXTRA].astype(jnp.int32).astype(F32)[:, 0:1]
        logits = near_half + xi[g, :, 0:width].astype(jnp.int32).astype(F32) * jnp.exp2(power - 15.0)
        masked = jnp.where(mask_ref[...] == 1, logits, jnp.float32(-1e30))
        local_max = jnp.max(masked, axis=1, keepdims=True)
        local_target = jnp.sum(jnp.where(onehot_of(g), logits, 0.0), axis=1, keepdims=True)
        local_sum = jnp.sum(jnp.exp(masked - local_max), axis=1, keepdims=True)
        lanes = lax.broadcasted_iota(jnp.int32, (m, 128), 1)
        packed = jnp.where(lanes == 0, local_max, jnp.where(lanes == 1, local_sum, local_target))
        if m < 128:
            packed = jnp.concatenate([packed, jnp.zeros((128 - m, 128), F32)], axis=0)
        mine = jnp.transpose(packed)[0:8]
        stats_out[g] = mine
        stats_in[g, me_v] = mine
        msk[g] = masked
        for k in range(1, nv):
            stat_copy(g, k).start()

    def grads_of(g):
        for k in range(1, nv):
            source = (me_v + nv - k) % nv
            rcopy(stats_out.at[g], stats_in.at[g, source], s_send.at[g, k], s_recv.at[g, source], source, me_t).wait_recv()
        row_max = stats_in[g, 0][0:1]
        for v in range(1, nv):
            row_max = jnp.maximum(row_max, stats_in[g, v][0:1])
        denominator = jnp.zeros_like(row_max)
        target_logit = jnp.zeros_like(row_max)
        for v in range(nv):
            got = stats_in[g, v]
            denominator += got[1:2] * jnp.exp(got[0:1] - row_max)
            target_logit += got[2:3]
        log_norm = row_max + jnp.log(denominator)
        loss_rows[g] = log_norm - target_logit
        column = jnp.transpose(jnp.broadcast_to(log_norm, (128, 128)))[0:m, 0:1]
        probabilities = jnp.exp(msk[g] - column)
        tok_grad = sides[g * m:(g + 1) * m, 1:2]
        dl[g, me_t] = (tok_grad * (probabilities - onehot_of(g).astype(F32))).astype(BF)
        grad_copy(g, 0).start()
        grad_copy(g, 1).start()

    def grads_on(g):
        t = tok_of(2)
        rcopy(dl.at[g, t], dl.at[g, t], d_send.at[g, 0], d_recv.at[g, 0], me_v, t).wait_recv()
        grad_copy(g, 2).start()

    def terms_of(g):
        for i, r in ((1, 1), (2, 3)):
            t = tok_of(r)
            rcopy(dl.at[g, t], dl.at[g, t], d_send.at[g, i], d_recv.at[g, i], me_v, tok_of(1)).wait_recv()
        lhs = dl[g].reshape(4 * m, width)
        for q in (1, 0):
            value = lax.dot_general(
                lhs, wbuf[weight_rows(q), :], (((1,), (1,)), ((), ())), preferred_element_type=F32
            ).reshape(4, m, feats)
            if q == 0:
                near[g] = value
            else:
                mix_out[g] = value.astype(BF)
                for r in (2, 3, 1, 0):
                    mix_copy(g, tok_of(r)).start()

    def mixed(g):
        for r in (2, 3, 1, 0):
            t = tok_of(r)
            mix_copy(g, t).wait_recv()
            both = (near[g, t] + mix_in[g, t].astype(F32)).astype(BF)
            if r == 0:
                @pl.when(home)
                def _():
                    fin[g, z] = both

                @pl.when(jnp.logical_not(home))
                def _():
                    eo[g, t] = both
                    far_copy(g, t).start()
            elif r == 1:
                eo[g, t] = both
                far_copy(g, t).start()
            else:
                eo[g, t] = both

                @pl.when(home)
                def _():
                    near_copy(g, t).start()

                @pl.when(jnp.logical_not(home))
                def _():
                    pass_copy(g, t).start()

    def relayed(g):
        for cc in range(2):
            @pl.when((1 - y) * 2 + cc != z)
            def _():
                rcopy(eo.at[g, 0], tin.at[g, cc], e_send.at[g, 0], t_recv.at[g, cc], me_v, (1 - y) * 2 + cc).wait_recv()
                relay_copy(g, cc).start()

    def finish(g):
        total = None
        for zz in range(4):
            @pl.when(jnp.logical_not(home & (z == zz)))
            def _():
                rcopy(eo.at[g, 0], fin.at[g, zz], e_send.at[g, 0], f_recv.at[g, zz], zz * 2 + x, me_t).wait_recv()
        for zz in range(4):
            term = fin[g, zz].astype(F32)
            total = term if total is None else total + term
        out_ref[pl.ds(g * m, m), :] = total.astype(BF)

    steps = (spread, logits_of, cross_over, softmax_of, grads_of, grads_on, terms_of, mixed, relayed, finish)
    for step, g in schedule(groups):
        steps[step - 1](g)

    loss_ref[...] = jnp.concatenate([loss_rows[g][:, 0:m] for g in range(groups)], axis=1)

    for g in range(groups):
        for k in (3, 2, 1):
            @pl.when(z + k < 4)
            def _():
                a_copy(g, z + k).wait_send()

            @pl.when(z - k >= 0)
            def _():
                a_copy(g, z - k).wait_send()

        @pl.when(jnp.logical_not(home))
        def _():
            a_copy(g, z).wait_send()

        for t in range(4):
            x_copy(g, t).wait_send()
            mix_copy(g, t).wait_send()

            @pl.when(jnp.logical_not(home & (me_t == t)))
            def _():
                pass_copy(g, t).wait_send()

        for k in range(2):
            pair_copy(g, k).wait_send()

            @pl.when((1 - y) * 2 + k != z)
            def _():
                relay_copy(g, k).wait_send()

        cross_copy(g).wait_send()
        for k in range(1, nv):
            stat_copy(g, k).wait_send()
        for i in range(3):
            grad_copy(g, i).wait_send()


def fused(vocab_size, tok_size):
    def on_device(hidden, head_weight, targets, vocab_mask, token_grad):
        rows, feats = hidden.shape
        width = head_weight.shape[1]
        groups = GROUPS
        m = rows // groups
        dma = pltpu.SemaphoreType.DMA
        vmem = pl.BlockSpec(memory_space=pltpu.VMEM)
        hbm = pl.BlockSpec(memory_space=pltpu.HBM)
        hidden_grad, loss = pl.pallas_call(
            lambda *refs: kernel(groups, *refs),
            out_shape=(
                jax.ShapeDtypeStruct((rows, feats), BF),
                jax.ShapeDtypeStruct((1, rows), F32),
            ),
            in_specs=[hbm, hbm] + [vmem] * 3,
            out_specs=(vmem, vmem),
            scratch_shapes=[
                pltpu.VMEM((groups, m, feats), BF),
                pltpu.VMEM((2 * feats, width), BF),
                pltpu.VMEM((2, groups, 4, m, feats), BF),
                pltpu.VMEM((groups, 4, m, width), F32),
                pltpu.VMEM((groups, 2, m, width), F32),
                pltpu.VMEM((groups, m, width + EXTRA), I16),
                pltpu.VMEM((groups, m, width + EXTRA), I16),
                pltpu.VMEM((groups, m, width), F32),
                pltpu.VMEM((groups, 8, 128), F32),
                pltpu.VMEM((groups, vocab_size, 8, 128), F32),
                pltpu.VMEM((groups, 1, 128), F32),
                pltpu.VMEM((groups, 4, m, width), BF),
                pltpu.VMEM((groups, 4, m, feats), BF),
                pltpu.VMEM((groups, 4, m, feats), BF),
                pltpu.VMEM((groups, 4, m, feats), F32),
                pltpu.VMEM((groups, 4, m, feats), BF),
                pltpu.VMEM((groups, 2, m, feats), BF),
                pltpu.VMEM((groups, 4, m, feats), BF),
                dma((groups,)), dma,
                dma((groups, 4)), dma((groups, 4)), dma((groups, 4)), dma((groups, 4)),
                dma((groups, 2)), dma((groups, 2)), dma((groups,)), dma((groups,)),
                dma((groups, 8)), dma((groups, 8)), dma((groups, 3)), dma((groups, 3)),
                dma((groups, 4)), dma((groups, 4)), dma((groups, 4)), dma((groups, 4)),
                dma((groups, 2)), dma((groups, 2)),
            ],
            compiler_params=pltpu.CompilerParams(
                collective_id=0, has_side_effects=True, vmem_limit_bytes=60 * 1024 * 1024
            ),
        )(hidden, head_weight, targets[None, :], vocab_mask[None, :], token_grad[None, :])
        return (hidden_grad, loss.reshape(rows))

    return on_device


def solution(mesh):
    placed = (P("tok", "vocab"), P("tok", "vocab"), P("tok"), P("vocab"), P("tok"))
    vocab_size, tok_size = mesh.shape["vocab"], mesh.shape["tok"]

    def body(hidden, head_weight, *rest):
        rows, feats = hidden.shape
        fits = tok_size == 4 and vocab_size == 8 and feats % 128 == 0 and head_weight.shape[1] % 256 == 0
        fits = fits and rows <= 256 and rows % (16 * GROUPS) == 0 and rows <= 128 * GROUPS
        build = fused if fits else make_on_device
        return build(vocab_size, tok_size)(hidden, head_weight, *rest)

    return jax.shard_map(
        body,
        mesh=mesh,
        in_specs=placed,
        out_specs=(P("tok", "vocab"), P("tok")),
        check_vma=False,
    )
```

time: 140 us -> 121 us (0.86); the launches traced: 140 us -> 119 us
  Pallas kernels: 137 us -> 115 us
    pallas_call x1, Pallas kernels: 137 us -> 115 us  [on_device(): pl.pallas_call(lambda *refs: kernel(groups, *refs), out_shape=(jax.ShapeD...]
where the time goes in v1:
time: 121 us; the launch traced here: 119 us
  Pallas kernels  115 us (95%)
  local copies, waits for them, and re-layouts  2.93 us (2%)
    pallas_call x1, Pallas kernels, on_device(): pl.pallas_call(lambda *refs: kernel(groups, *refs), out_shape=(jax.ShapeD...  115 us
    unnamed x2, local copies, waits for them, and re-layouts  2.93 us

profile of v1, /device:TPU:0, one launch (start us, length us, event | category | flops | bytes accessed | tf_op | source)
XLA Modules:
  0.0 119.1 jit_solution(4379749195585949343)
XLA Ops:
  0.6 115.5 %shard_map.68 = (bf16[192,896]{1,0:T(8,128)(2,1)}, f32[1,192]{1,0:T(1,128)}) custom-call(bf16[192,896]{1,0:T(8,128)(2,1)} %refs_0_.1, bf16[1792,1024]{1,0:T(8,128)(2,1)} %refs_1_.1, s32[1,192]{1,0:T(1,128)} %bitcast.5, s32[1,1024]{1,0:T(1,128)} %bitcast.4, f32[1,192]{1,0:T(1,128)} %bitcast.6), custom_call_target="tpu_custom_call" | custom-call | tf_op jit(solution)/shard_map/pallas_call | solution.py:411
  116.1 1.7 %copy.9 = bf16[192,896]{1,0:T(8,128)(2,1)} copy(bf16[192,896]{1,0:T(8,128)(2,1)} %get-tuple-element.8) | data formatting | bytes 688128
  117.9 1.2 %copy.10 = f32[192]{0:T(256)} copy(f32[192]{0:T(256)} %bitcast.7) | data formatting | bytes 1536

commit v2 on v1

--- a/solution.py
+++ b/solution.py
@@ -64,27 +64,22 @@
     return on_device
 
 
-GROUPS = 3
+SIZES = (64, 64, 64)
 EXTRA = 128
 BF = jnp.bfloat16
 F32 = jnp.float32
 I16 = jnp.int16
 
 
-def schedule(groups):
-    period, base = 29.5 / groups, 11.0
-    took = {1: 0.0, 2: 3.0, 3: 3.0, 4: 3.0 + 8.4 / groups, 5: 4.7, 6: 2.2 + 8.4 / groups, 7: 1.3, 8: 4.5, 9: 4.5, 10: 4.5}
-    events = []
-    for g in range(groups):
-        at = base + period * (g + 1)
-        for step in range(1, 11):
-            at += took[step]
-            events.append((at, step, g))
-    return [(step, g) for _, step, g in sorted(events)]
+PLAN = """
+ga0 ga1 sp0 ga2 sp1 lg0 co0 sp2 lg1 sm0 co1 gr0 lg2 sm1 go0 co2
+tm0 gr1 sm2 go1 m20 m30 tm1 m10 m00 r00 r10 gr2 m21 m31 go2 tm2
+m11 m01 r01 r11 fi0 m22 m32 m12 m02 r02 r12 fi1 fi2
+"""
 
 
 def kernel(
-    groups,
+    sizes,
     hidden_ref, weight_ref, targets_ref, mask_ref, grad_ref,
     out_ref, loss_ref,
     hid, wbuf, hb, plog, pin, xo, xi, msk, stats_out, stats_in, loss_rows, dl,
@@ -93,7 +88,8 @@
     s_send, s_recv, d_send, d_recv, m_send, m_recv, e_send, f_recv, t_recv, r_send,
 ):
     rows, feats = hidden_ref.shape
-    m = rows // groups
+    groups = len(sizes)
+    firsts = [sum(sizes[:g]) for g in range(groups)]
     width = weight_ref.shape[1]
     me_v = lax.axis_index("vocab")
     me_t = lax.axis_index("tok")
@@ -115,7 +111,10 @@
             device_id=dev(v, t), device_id_type=pl.DeviceIdType.MESH,
         )
 
-    loads = [pltpu.make_async_copy(hidden_ref.at[pl.ds(g * m, m)], hid.at[g], l_sem.at[g]) for g in range(groups)]
+    def span(g):
+        return pl.ds(firsts[g], sizes[g])
+
+    loads = [pltpu.make_async_copy(hidden_ref.at[span(g)], hid.at[span(g)], l_sem.at[g]) for g in range(groups)]
     for load in loads:
         load.start()
     weights = pltpu.make_async_copy(weight_ref, wbuf, w_sem)
@@ -136,17 +135,17 @@
     home = me_t == z
 
     def a_copy(g, zz):
-        return rcopy(hid.at[g], hb.at[0, g, me_t], a_send.at[g, zz], a_recv.at[g, me_t], zz * 2 + x, z)
+        return rcopy(hid.at[span(g)], hb.at[0, me_t, span(g)], a_send.at[g, zz], a_recv.at[g, me_t], zz * 2 + x, z)
 
     def x_copy(g, t):
-        return rcopy(hb.at[0, g, t], hb.at[1, g, t], x_send.at[g, t], x_recv.at[g, t], other_x, me_t)
+        return rcopy(hb.at[0, t, span(g)], hb.at[1, t, span(g)], x_send.at[g, t], x_recv.at[g, t], other_x, me_t)
 
     def x_own(g):
-        return rcopy(hid.at[g], hb.at[1, g, me_t], x_send.at[g, me_t], x_recv.at[g, me_t], other_x, me_t)
-
-    for g in range(groups):
+        return rcopy(hid.at[span(g)], hb.at[1, me_t, span(g)], x_send.at[g, me_t], x_recv.at[g, me_t], other_x, me_t)
+
+    def gather(g):
         loads[g].wait()
-        for k in (3, 2, 1):
+        for k in (1, 2, 3):
             @pl.when(z + k < 4)
             def _():
                 a_copy(g, z + k).start()
@@ -163,58 +162,58 @@
         def _():
             x_own(g).start()
 
-    @pl.when(home)
-    def _():
-        for g in range(groups):
-            hb[0, g, me_t] = hid[g]
 
     top = jnp.concatenate([targets_ref[...].astype(F32), grad_ref[...]], axis=0)
     top = jnp.concatenate([top, jnp.zeros((2, 256 - rows), F32)], axis=1)
     sides = jnp.transpose(jnp.concatenate([top, jnp.zeros((126, 256), F32)], axis=0))
-    columns = me_v * width + lax.broadcasted_iota(jnp.int32, (m, width), 1)
 
     def onehot_of(g):
-        return columns == sides[g * m:(g + 1) * m, 0:1].astype(jnp.int32)
+        columns = me_v * width + lax.broadcasted_iota(jnp.int32, (sizes[g], width), 1)
+        return columns == sides[firsts[g]:firsts[g] + sizes[g], 0:1].astype(jnp.int32)
 
     def weight_rows(q):
         owner = (x + q) % 2
         return pl.ds(pl.multiple_of(owner * feats, 128), feats)
 
     def pair_copy(g, k):
-        return rcopy(plog.at[g, tok_of(1 + 2 * k)], pin.at[g, k], p_send.at[g, k], p_recv.at[g, k], me_v, tok_of(1))
+        return rcopy(plog.at[tok_of(1 + 2 * k), span(g)], pin.at[k, span(g)], p_send.at[g, k], p_recv.at[g, k], me_v, tok_of(1))
 
     def cross_copy(g):
-        return rcopy(xo.at[g], xi.at[g], c_send.at[g], c_recv.at[g], me_v, tok_of(2))
+        return rcopy(xo.at[span(g)], xi.at[span(g)], c_send.at[g], c_recv.at[g], me_v, tok_of(2))
 
     def stat_copy(g, k):
         return rcopy(stats_out.at[g], stats_in.at[g, me_v], s_send.at[g, k], s_recv.at[g, me_v], (me_v + k) % nv, me_t)
 
     def grad_copy(g, i):
         t = tok_of(2) if i == 2 else me_t
-        return rcopy(dl.at[g, t], dl.at[g, t], d_send.at[g, i], d_recv.at[g, i], me_v, tok_of(2 if i == 0 else 1))
+        return rcopy(dl.at[t, span(g)], dl.at[t, span(g)], d_send.at[g, i], d_recv.at[g, i], me_v, tok_of(2 if i == 0 else 1))
 
     def mix_copy(g, t):
-        return rcopy(mix_out.at[g, t], mix_in.at[g, t], m_send.at[g, t], m_recv.at[g, t], other_x, me_t)
+        return rcopy(mix_out.at[t, span(g)], mix_in.at[t, span(g)], m_send.at[g, t], m_recv.at[g, t], other_x, me_t)
 
     def pass_copy(g, t):
-        return rcopy(eo.at[g, t], tin.at[g, c], e_send.at[g, t], t_recv.at[g, c], me_v, t)
+        return rcopy(eo.at[t, span(g)], tin.at[c, span(g)], e_send.at[g, t], t_recv.at[g, c], me_v, t)
 
     def near_copy(g, t):
-        return rcopy(eo.at[g, t], fin.at[g, z], e_send.at[g, t], f_recv.at[g, z], me_v, t)
+        return rcopy(eo.at[t, span(g)], fin.at[z, span(g)], e_send.at[g, t], f_recv.at[g, z], me_v, t)
 
     def far_copy(g, t):
-        return rcopy(eo.at[g, t], fin.at[g, z], e_send.at[g, t], f_recv.at[g, z], me_t * 2 + x, t)
+        return rcopy(eo.at[t, span(g)], fin.at[z, span(g)], e_send.at[g, t], f_recv.at[g, z], me_t * 2 + x, t)
 
     def relay_copy(g, cc):
-        return rcopy(tin.at[g, cc], fin.at[g, z], r_send.at[g, cc], f_recv.at[g, z], ((1 - y) * 2 + cc) * 2 + x, me_t)
+        return rcopy(tin.at[cc, span(g)], fin.at[z, span(g)], r_send.at[g, cc], f_recv.at[g, z], ((1 - y) * 2 + cc) * 2 + x, me_t)
 
     tile = 256
 
     def spread(g):
+        @pl.when(home)
+        def _():
+            hb[0, me_t, span(g)] = hid[span(g)]
+
         for t in range(4):
             @pl.when(jnp.logical_not(home & (me_t == t)))
             def _():
-                a_copy_in = rcopy(hid.at[g], hb.at[0, g, t], a_send.at[g, 0], a_recv.at[g, t], me_v, t)
+                a_copy_in = rcopy(hid.at[span(g)], hb.at[0, t, span(g)], a_send.at[g, 0], a_recv.at[g, t], me_v, t)
                 a_copy_in.wait_recv()
                 x_copy(g, t).start()
 
@@ -229,34 +228,35 @@
             cols = pl.ds(pl.multiple_of(j * tile, tile), tile)
             total = None
             for q in range(2):
-                lhs = hb[q, g].reshape(4 * m, feats)
+                lhs = hb[q, :, span(g), :].reshape(4 * sizes[g], feats)
                 term = jnp.dot(lhs, wbuf[weight_rows(q), cols], preferred_element_type=F32)
                 total = term if total is None else total + term
-            plog[g, :, :, cols] = total.reshape(4, m, tile)
+            plog[:, span(g), cols] = total.reshape(4, sizes[g], tile)
 
         pair_copy(g, 1).start()
         pair_copy(g, 0).start()
 
     def cross_over(g):
         pair_copy(g, 1).wait_recv()
-        value = plog[g, tok_of(2)] + pin[g, 1]
+        value = plog[tok_of(2), span(g), :] + pin[1, span(g), :]
         top_of = jnp.max(jnp.abs(value), axis=1, keepdims=True)
         power = jnp.ceil(jnp.log2(jnp.maximum(top_of, jnp.float32(1e-20))) + jnp.float32(0.001))
         coded = jnp.round(value * jnp.exp2(15.0 - power)).astype(jnp.int32)
-        xo[g, :, 0:width] = coded.astype(I16)
-        xo[g, :, width:width + EXTRA] = jnp.broadcast_to(power.astype(jnp.int32), (m, EXTRA)).astype(I16)
+        xo[span(g), 0:width] = coded.astype(I16)
+        xo[span(g), width:width + EXTRA] = jnp.broadcast_to(power.astype(jnp.int32), (sizes[g], EXTRA)).astype(I16)
         cross_copy(g).start()
 
     def softmax_of(g):
         pair_copy(g, 0).wait_recv()
-        near_half = plog[g, me_t] + pin[g, 0]
+        near_half = plog[me_t, span(g), :] + pin[0, span(g), :]
         cross_copy(g).wait_recv()
-        power = xi[g, :, width:width + EXTRA].astype(jnp.int32).astype(F32)[:, 0:1]
-        logits = near_half + xi[g, :, 0:width].astype(jnp.int32).astype(F32) * jnp.exp2(power - 15.0)
+        power = xi[span(g), width:width + EXTRA].astype(jnp.int32).astype(F32)[:, 0:1]
+        logits = near_half + xi[span(g), 0:width].astype(jnp.int32).astype(F32) * jnp.exp2(power - 15.0)
         masked = jnp.where(mask_ref[...] == 1, logits, jnp.float32(-1e30))
         local_max = jnp.max(masked, axis=1, keepdims=True)
         local_target = jnp.sum(jnp.where(onehot_of(g), logits, 0.0), axis=1, keepdims=True)
         local_sum = jnp.sum(jnp.exp(masked - local_max), axis=1, keepdims=True)
+        m = sizes[g]
         lanes = lax.broadcasted_iota(jnp.int32, (m, 128), 1)
         packed = jnp.where(lanes == 0, local_max, jnp.where(lanes == 1, local_sum, local_target))
         if m < 128:
@@ -264,7 +264,7 @@
         mine = jnp.transpose(packed)[0:8]
         stats_out[g] = mine
         stats_in[g, me_v] = mine
-        msk[g] = masked
+        msk[span(g), :] = masked
         for k in range(1, nv):
             stat_copy(g, k).start()
 
@@ -283,85 +283,92 @@
             target_logit += got[2:3]
         log_norm = row_max + jnp.log(denominator)
         loss_rows[g] = log_norm - target_logit
-        column = jnp.transpose(jnp.broadcast_to(log_norm, (128, 128)))[0:m, 0:1]
-        probabilities = jnp.exp(msk[g] - column)
-        tok_grad = sides[g * m:(g + 1) * m, 1:2]
-        dl[g, me_t] = (tok_grad * (probabilities - onehot_of(g).astype(F32))).astype(BF)
+        column = jnp.transpose(jnp.broadcast_to(log_norm, (128, 128)))[0:sizes[g], 0:1]
+        probabilities = jnp.exp(msk[span(g), :] - column)
+        tok_grad = sides[firsts[g]:firsts[g] + sizes[g], 1:2]
+        dl[me_t, span(g), :] = (tok_grad * (probabilities - onehot_of(g).astype(F32))).astype(BF)
         grad_copy(g, 0).start()
         grad_copy(g, 1).start()
 
     def grads_on(g):
         t = tok_of(2)
-        rcopy(dl.at[g, t], dl.at[g, t], d_send.at[g, 0], d_recv.at[g, 0], me_v, t).wait_recv()
+        rcopy(dl.at[t, span(g)], dl.at[t, span(g)], d_send.at[g, 0], d_recv.at[g, 0], me_v, t).wait_recv()
         grad_copy(g, 2).start()
 
     def terms_of(g):
         for i, r in ((1, 1), (2, 3)):
             t = tok_of(r)
-            rcopy(dl.at[g, t], dl.at[g, t], d_send.at[g, i], d_recv.at[g, i], me_v, tok_of(1)).wait_recv()
-        lhs = dl[g].reshape(4 * m, width)
+            rcopy(dl.at[t, span(g)], dl.at[t, span(g)], d_send.at[g, i], d_recv.at[g, i], me_v, tok_of(1)).wait_recv()
+        lhs = dl[:, span(g), :].reshape(4 * sizes[g], width)
         for q in (1, 0):
             value = lax.dot_general(
                 lhs, wbuf[weight_rows(q), :], (((1,), (1,)), ((), ())), preferred_element_type=F32
-            ).reshape(4, m, feats)
+            ).reshape(4, sizes[g], feats)
             if q == 0:
-                near[g] = value
+                near[:, span(g), :] = value
             else:
-                mix_out[g] = value.astype(BF)
+                mix_out[:, span(g), :] = value.astype(BF)
                 for r in (2, 3, 1, 0):
                     mix_copy(g, tok_of(r)).start()
 
-    def mixed(g):
-        for r in (2, 3, 1, 0):
-            t = tok_of(r)
-            mix_copy(g, t).wait_recv()
-            both = (near[g, t] + mix_in[g, t].astype(F32)).astype(BF)
-            if r == 0:
-                @pl.when(home)
-                def _():
-                    fin[g, z] = both
-
-                @pl.when(jnp.logical_not(home))
-                def _():
-                    eo[g, t] = both
-                    far_copy(g, t).start()
-            elif r == 1:
-                eo[g, t] = both
+    def mixed(g, r):
+        t = tok_of(r)
+        mix_copy(g, t).wait_recv()
+        both = (near[t, span(g), :] + mix_in[t, span(g), :].astype(F32)).astype(BF)
+        if r == 0:
+            @pl.when(home)
+            def _():
+                fin[z, span(g), :] = both
+
+            @pl.when(jnp.logical_not(home))
+            def _():
+                eo[t, span(g), :] = both
                 far_copy(g, t).start()
-            else:
-                eo[g, t] = both
-
-                @pl.when(home)
-                def _():
-                    near_copy(g, t).start()
-
-                @pl.when(jnp.logical_not(home))
-                def _():
-                    pass_copy(g, t).start()
-
-    def relayed(g):
-        for cc in range(2):
-            @pl.when((1 - y) * 2 + cc != z)
-            def _():
-                rcopy(eo.at[g, 0], tin.at[g, cc], e_send.at[g, 0], t_recv.at[g, cc], me_v, (1 - y) * 2 + cc).wait_recv()
-                relay_copy(g, cc).start()
+        elif r == 1:
+            eo[t, span(g), :] = both
+            far_copy(g, t).start()
+        else:
+            eo[t, span(g), :] = both
+
+            @pl.when(home)
+            def _():
+                near_copy(g, t).start()
+
+            @pl.when(jnp.logical_not(home))
+            def _():
+                pass_copy(g, t).start()
+
+    def relayed(g, r):
+        cc = (c + r) % 2
+
+        @pl.when((1 - y) * 2 + cc != z)
+        def _():
+            rcopy(eo.at[0, span(g)], tin.at[cc, span(g)], e_send.at[g, 0], t_recv.at[g, cc], me_v, (1 - y) * 2 + cc).wait_recv()
+            relay_copy(g, cc).start()
 
     def finish(g):
         total = None
         for zz in range(4):
             @pl.when(jnp.logical_not(home & (z == zz)))
             def _():
-                rcopy(eo.at[g, 0], fin.at[g, zz], e_send.at[g, 0], f_recv.at[g, zz], zz * 2 + x, me_t).wait_recv()
+                rcopy(eo.at[0, span(g)], fin.at[zz, span(g)], e_send.at[g, 0], f_recv.at[g, zz], zz * 2 + x, me_t).wait_recv()
         for zz in range(4):
-            term = fin[g, zz].astype(F32)
+            term = fin[zz, span(g), :].astype(F32)
             total = term if total is None else total + term
-        out_ref[pl.ds(g * m, m), :] = total.astype(BF)
-
-    steps = (spread, logits_of, cross_over, softmax_of, grads_of, grads_on, terms_of, mixed, relayed, finish)
-    for step, g in schedule(groups):
-        steps[step - 1](g)
-
-    loss_ref[...] = jnp.concatenate([loss_rows[g][:, 0:m] for g in range(groups)], axis=1)
+        out_ref[span(g), :] = total.astype(BF)
+
+    steps = {
+        "ga": gather, "sp": spread, "lg": logits_of, "co": cross_over, "sm": softmax_of, "gr": grads_of, "go": grads_on,
+        "tm": terms_of, "fi": finish,
+    }
+    for r in range(4):
+        steps[f"m{r}"] = lambda g, r=r: mixed(g, r)
+    for r in range(2):
+        steps[f"r{r}"] = lambda g, r=r: relayed(g, r)
+    for item in PLAN.split():
+        steps[item[:2]](int(item[2:]))
+
+    loss_ref[...] = jnp.concatenate([loss_rows[g][:, 0:sizes[g]] for g in range(groups)], axis=1)
 
     for g in range(groups):
         for k in (3, 2, 1):
@@ -403,13 +410,12 @@
     def on_device(hidden, head_weight, targets, vocab_mask, token_grad):
         rows, feats = hidden.shape
         width = head_weight.shape[1]
-        groups = GROUPS
-        m = rows // groups
+        groups = len(SIZES)
         dma = pltpu.SemaphoreType.DMA
         vmem = pl.BlockSpec(memory_space=pltpu.VMEM)
         hbm = pl.BlockSpec(memory_space=pltpu.HBM)
         hidden_grad, loss = pl.pallas_call(
-            lambda *refs: kernel(groups, *refs),
+            lambda *refs: kernel(SIZES, *refs),
             out_shape=(
                 jax.ShapeDtypeStruct((rows, feats), BF),
                 jax.ShapeDtypeStruct((1, rows), F32),
@@ -417,24 +423,24 @@
             in_specs=[hbm, hbm] + [vmem] * 3,
             out_specs=(vmem, vmem),
             scratch_shapes=[
-                pltpu.VMEM((groups, m, feats), BF),
+                pltpu.VMEM((rows, feats), BF),
                 pltpu.VMEM((2 * feats, width), BF),
-                pltpu.VMEM((2, groups, 4, m, feats), BF),
-                pltpu.VMEM((groups, 4, m, width), F32),
-                pltpu.VMEM((groups, 2, m, width), F32),
-                pltpu.VMEM((groups, m, width + EXTRA), I16),
-                pltpu.VMEM((groups, m, width + EXTRA), I16),
-                pltpu.VMEM((groups, m, width), F32),
+                pltpu.VMEM((2, 4, rows, feats), BF),
+                pltpu.VMEM((4, rows, width), F32),
+                pltpu.VMEM((2, rows, width), F32),
+                pltpu.VMEM((rows, width + EXTRA), I16),
+                pltpu.VMEM((rows, width + EXTRA), I16),
+                pltpu.VMEM((rows, width), F32),
                 pltpu.VMEM((groups, 8, 128), F32),
                 pltpu.VMEM((groups, vocab_size, 8, 128), F32),
                 pltpu.VMEM((groups, 1, 128), F32),
-                pltpu.VMEM((groups, 4, m, width), BF),
-                pltpu.VMEM((groups, 4, m, feats), BF),
-                pltpu.VMEM((groups, 4, m, feats), BF),
-                pltpu.VMEM((groups, 4, m, feats), F32),
-                pltpu.VMEM((groups, 4, m, feats), BF),
-                pltpu.VMEM((groups, 2, m, feats), BF),
-                pltpu.VMEM((groups, 4, m, feats), BF),
+                pltpu.VMEM((4, rows, width), BF),
+                pltpu.VMEM((4, rows, feats), BF),
+                pltpu.VMEM((4, rows, feats), BF),
+                pltpu.VMEM((4, rows, feats), F32),
+                pltpu.VMEM((4, rows, feats), BF),
+                pltpu.VMEM((2, rows, feats), BF),
+                pltpu.VMEM((4, rows, feats), BF),
                 dma((groups,)), dma,
                 dma((groups, 4)), dma((groups, 4)), dma((groups, 4)), dma((groups, 4)),
                 dma((groups, 2)), dma((groups, 2)), dma((groups,)), dma((groups,)),
@@ -458,7 +464,7 @@
     def body(hidden, head_weight, *rest):
         rows, feats = hidden.shape
         fits = tok_size == 4 and vocab_size == 8 and feats % 128 == 0 and head_weight.shape[1] % 256 == 0
-        fits = fits and rows <= 256 and rows % (16 * GROUPS) == 0 and rows <= 128 * GROUPS
+        fits = fits and rows <= 256 and rows == sum(SIZES)
         build = fused if fits else make_on_device
         return build(vocab_size, tok_size)(hidden, head_weight, *rest)
 

time: 121 us -> 104 us (0.86); the launches traced: 119 us -> 104 us
  Pallas kernels: 115 us -> 100 us
    pallas_call x1, Pallas kernels: 115 us -> 100 us  [on_device(): pl.pallas_call(lambda *refs: kernel(SIZES, *refs), out_shape=(jax.ShapeDt...]
where the time goes in v2:
time: 104 us
  Pallas kernels  100 us (96%)
  local copies, waits for them, and re-layouts  2.93 us (3%)
    pallas_call x1, Pallas kernels, on_device(): pl.pallas_call(lambda *refs: kernel(SIZES, *refs), out_shape=(jax.ShapeDt...  100 us
    unnamed x2, local copies, waits for them, and re-layouts  2.93 us

profile of v2, /device:TPU:0, one launch (start us, length us, event | category | flops | bytes accessed | tf_op | source)
XLA Modules:
  0.0 103.6 jit_solution(15390666666190295808)
XLA Ops:
  0.6 100.0 %shard_map.68 = (bf16[192,896]{1,0:T(8,128)(2,1)}, f32[1,192]{1,0:T(1,128)}) custom-call(bf16[192,896]{1,0:T(8,128)(2,1)} %refs_0_.1, bf16[1792,1024]{1,0:T(8,128)(2,1)} %refs_1_.1, s32[1,192]{1,0:T(1,128)} %bitcast.5, s32[1,1024]{1,0:T(1,128)} %bitcast.4, f32[1,192]{1,0:T(1,128)} %bitcast.6), custom_call_target="tpu_custom_call" | custom-call | tf_op jit(solution)/shard_map/pallas_call | solution.py:417
  100.7 1.7 %copy.9 = bf16[192,896]{1,0:T(8,128)(2,1)} copy(bf16[192,896]{1,0:T(8,128)(2,1)} %get-tuple-element.8) | data formatting | bytes 688128
  102.4 1.2 %copy.10 = f32[192]{0:T(256)} copy(f32[192]{0:T(256)} %bitcast.7) | data formatting | bytes 1536

commit v3 on v2

--- a/solution.py
+++ b/solution.py
@@ -64,27 +64,29 @@
     return on_device
 
 
-SIZES = (64, 64, 64)
+SIZES = (32, 48, 48, 64)
 EXTRA = 128
 BF = jnp.bfloat16
 F32 = jnp.float32
 I16 = jnp.int16
 
 
-PLAN = """
-ga0 ga1 sp0 ga2 sp1 lg0 co0 sp2 lg1 sm0 co1 gr0 lg2 sm1 go0 co2
-tm0 gr1 sm2 go1 m20 m30 tm1 m10 m00 r00 r10 gr2 m21 m31 go2 tm2
-m11 m01 r01 r11 fi0 m22 m32 m12 m02 r02 r12 fi1 fi2
-"""
+PLAN = (
+    "ga0", "ga1", "ld0", "ld1", "sp0", "ga2", "ga3", "ld2", "sp1", "sp2", "lg0", "ld3", "co0", "lg1", "sm0",
+    "co1", "sp3", "lg2", "sm1", "co2", "gr0", "go0", "sm2", "tm0", "gr1", "lg3", "gr2", "m30", "m20", "go1",
+    "tm1", "co3", "m10", "go2", "r00", "m00", "r10", "sm3", "m31", "m21", "m11", "r11", "tm2", "gr3", "r01",
+    "m22", "m01", "go3", "tm3", "m32", "m12", "r02", "m23", "r12", "m02", "fi1", "m13", "m33", "r03", "r13",
+    "fi2", "m03", "fi0", "fi3",
+)
 
 
 def kernel(
     sizes,
     hidden_ref, weight_ref, targets_ref, mask_ref, grad_ref,
     out_ref, loss_ref,
-    hid, wbuf, hb, plog, pin, xo, xi, msk, stats_out, stats_in, loss_rows, dl,
+    hid, wbuf, land, hb, plog, pin, xo, xi, msk, stats_out, stats_in, loss_rows, dl,
     mix_out, mix_in, near, eo, tin, fin,
-    l_sem, w_sem, a_send, a_recv, x_send, x_recv, p_send, p_recv, c_send, c_recv,
+    l_sem, w_sem, a_send, a_recv, n_recv, n_send, x_send, x_recv, p_send, p_recv, c_send, c_recv,
     s_send, s_recv, d_send, d_recv, m_send, m_recv, e_send, f_recv, t_recv, r_send,
 ):
     rows, feats = hidden_ref.shape
@@ -134,8 +136,36 @@
 
     home = me_t == z
 
-    def a_copy(g, zz):
-        return rcopy(hid.at[span(g)], hb.at[0, me_t, span(g)], a_send.at[g, zz], a_recv.at[g, me_t], zz * 2 + x, z)
+    side = z // 2
+    partner = z + 1 - 2 * (z % 2)
+    inner = jnp.where(z < 2, 2, 1)
+    outer = jnp.where(z < 2, 0, 3)
+    is_inner = (z == 1) | (z == 2)
+    landed = is_inner & (me_t // 2 == 1 - side)
+
+    def a_copy(g):
+        return rcopy(hid.at[span(g)], hb.at[0, me_t, span(g)], a_send.at[g, 0], a_recv.at[g, me_t], partner * 2 + x, z)
+
+    def n_copy(g):
+        i = jnp.where(is_inner, 0, 1)
+        return rcopy(hid.at[span(g)], land.at[i, span(g)], a_send.at[g, 1], n_recv.at[g, i], inner * 2 + x, me_t)
+
+    def o_copy(g):
+        return rcopy(hid.at[span(g)], hb.at[0, me_t, span(g)], a_send.at[g, 2], a_recv.at[g, me_t], me_v, z)
+
+    def landing(i):
+        return jnp.where(z == 2, 1 - i, 2 + i)
+
+    def n_out(g, i):
+        return rcopy(
+            land.at[i, span(g)], hb.at[0, me_t, span(g)], n_send.at[g, i, 0], a_recv.at[g, me_t], outer * 2 + x, landing(i)
+        )
+
+    def n_near(g, i):
+        return rcopy(land.at[i, span(g)], hb.at[0, me_t, span(g)], n_send.at[g, i, 1], a_recv.at[g, me_t], me_v, landing(i))
+
+    def n_own(g, i):
+        return rcopy(land.at[i, span(g)], hb.at[1, me_t, span(g)], x_send.at[g, me_t], x_recv.at[g, me_t], other_x, me_t)
 
     def x_copy(g, t):
         return rcopy(hb.at[0, t, span(g)], hb.at[1, t, span(g)], x_send.at[g, t], x_recv.at[g, t], other_x, me_t)
@@ -145,18 +175,12 @@
 
     def gather(g):
         loads[g].wait()
-        for k in (1, 2, 3):
-            @pl.when(z + k < 4)
-            def _():
-                a_copy(g, z + k).start()
-
-            @pl.when(z - k >= 0)
-            def _():
-                a_copy(g, z - k).start()
+        a_copy(g).start()
+        n_copy(g).start()
 
         @pl.when(jnp.logical_not(home))
         def _():
-            a_copy(g, z).start()
+            o_copy(g).start()
 
         @pl.when(home)
         def _():
@@ -205,13 +229,31 @@
 
     tile = 256
 
+    def passed(g):
+        @pl.when(is_inner)
+        def _():
+            for i in range(2):
+                rcopy(
+                    hid.at[span(g)], land.at[i, span(g)], a_send.at[g, 1], n_recv.at[g, i], landing(i) * 2 + x, me_t
+                ).wait_recv()
+                n_out(g, i).start()
+
+                @pl.when(landing(i) != me_t)
+                def _():
+                    n_near(g, i).start()
+
+                @pl.when(landing(i) == me_t)
+                def _():
+                    n_own(g, i).start()
+                    hb[0, me_t, span(g)] = land[i, span(g)]
+
     def spread(g):
         @pl.when(home)
         def _():
             hb[0, me_t, span(g)] = hid[span(g)]
 
         for t in range(4):
-            @pl.when(jnp.logical_not(home & (me_t == t)))
+            @pl.when(jnp.logical_not((home | landed) & (me_t == t)))
             def _():
                 a_copy_in = rcopy(hid.at[span(g)], hb.at[0, t, span(g)], a_send.at[g, 0], a_recv.at[g, t], me_v, t)
                 a_copy_in.wait_recv()
@@ -358,31 +400,34 @@
         out_ref[span(g), :] = total.astype(BF)
 
     steps = {
-        "ga": gather, "sp": spread, "lg": logits_of, "co": cross_over, "sm": softmax_of, "gr": grads_of, "go": grads_on,
+        "ga": gather, "ld": passed, "sp": spread, "lg": logits_of, "co": cross_over, "sm": softmax_of, "gr": grads_of, "go": grads_on,
         "tm": terms_of, "fi": finish,
     }
     for r in range(4):
         steps[f"m{r}"] = lambda g, r=r: mixed(g, r)
     for r in range(2):
         steps[f"r{r}"] = lambda g, r=r: relayed(g, r)
-    for item in PLAN.split():
+    for item in PLAN:
         steps[item[:2]](int(item[2:]))
 
     loss_ref[...] = jnp.concatenate([loss_rows[g][:, 0:sizes[g]] for g in range(groups)], axis=1)
 
     for g in range(groups):
-        for k in (3, 2, 1):
-            @pl.when(z + k < 4)
-            def _():
-                a_copy(g, z + k).wait_send()
-
-            @pl.when(z - k >= 0)
-            def _():
-                a_copy(g, z - k).wait_send()
+        a_copy(g).wait_send()
+        n_copy(g).wait_send()
 
         @pl.when(jnp.logical_not(home))
         def _():
-            a_copy(g, z).wait_send()
+            o_copy(g).wait_send()
+
+        @pl.when(is_inner)
+        def _():
+            for i in range(2):
+                n_out(g, i).wait_send()
+
+                @pl.when(landing(i) != me_t)
+                def _():
+                    n_near(g, i).wait_send()
 
         for t in range(4):
             x_copy(g, t).wait_send()
@@ -425,6 +470,7 @@
             scratch_shapes=[
                 pltpu.VMEM((rows, feats), BF),
                 pltpu.VMEM((2 * feats, width), BF),
+                pltpu.VMEM((2, rows, feats), BF),
                 pltpu.VMEM((2, 4, rows, feats), BF),
                 pltpu.VMEM((4, rows, width), F32),
                 pltpu.VMEM((2, rows, width), F32),
@@ -442,7 +488,7 @@
                 pltpu.VMEM((2, rows, feats), BF),
                 pltpu.VMEM((4, rows, feats), BF),
                 dma((groups,)), dma,
-                dma((groups, 4)), dma((groups, 4)), dma((groups, 4)), dma((groups, 4)),
+                dma((groups, 3)), dma((groups, 4)), dma((groups, 2)), dma((groups, 2, 2)), dma((groups, 4)), dma((groups, 4)),
                 dma((groups, 2)), dma((groups, 2)), dma((groups,)), dma((groups,)),
                 dma((groups, 8)), dma((groups, 8)), dma((groups, 3)), dma((groups, 3)),
                 dma((groups, 4)), dma((groups, 4)), dma((groups, 4)), dma((groups, 4)),

time: 104 us -> 100 us (0.962)
  Pallas kernels: 100 us -> 96.5 us
    pallas_call x1, Pallas kernels: 100 us -> 96.5 us  [on_device(): pl.pallas_call(lambda *refs: kernel(SIZES, *refs), out_shape=(jax.ShapeDt...]
where the time goes in v3:
time: 100 us
  Pallas kernels  96.5 us (96%)
  local copies, waits for them, and re-layouts  2.93 us (3%)
    pallas_call x1, Pallas kernels, on_device(): pl.pallas_call(lambda *refs: kernel(SIZES, *refs), out_shape=(jax.ShapeDt...  96.5 us
    unnamed x2, local copies, waits for them, and re-layouts  2.93 us

profile of v3, /device:TPU:0, one launch (start us, length us, event | category | flops | bytes accessed | tf_op | source)
XLA Modules:
  0.0 100.1 jit_solution(13314627668927721439)
XLA Ops:
  0.6 96.5 %shard_map.68 = (bf16[192,896]{1,0:T(8,128)(2,1)}, f32[1,192]{1,0:T(1,128)}) custom-call(bf16[192,896]{1,0:T(8,128)(2,1)} %refs_0_.1, bf16[1792,1024]{1,0:T(8,128)(2,1)} %refs_1_.1, s32[1,192]{1,0:T(1,128)} %bitcast.5, s32[1,1024]{1,0:T(1,128)} %bitcast.4, f32[1,192]{1,0:T(1,128)} %bitcast.6), custom_call_target="tpu_custom_call" | custom-call | tf_op jit(solution)/shard_map/pallas_call | solution.py:462
  97.2 1.7 %copy.9 = bf16[192,896]{1,0:T(8,128)(2,1)} copy(bf16[192,896]{1,0:T(8,128)(2,1)} %get-tuple-element.8) | data formatting | bytes 688128
  98.9 1.2 %copy.10 = f32[192]{0:T(256)} copy(f32[192]{0:T(256)} %bitcast.7) | data formatting | bytes 1536

commit v4 on v3

--- a/solution.py
+++ b/solution.py
@@ -64,7 +64,7 @@
     return on_device
 
 
-SIZES = (32, 48, 48, 64)
+SIZES = (48, 48, 48, 48)
 EXTRA = 128
 BF = jnp.bfloat16
 F32 = jnp.float32
@@ -72,11 +72,11 @@
 
 
 PLAN = (
-    "ga0", "ga1", "ld0", "ld1", "sp0", "ga2", "ga3", "ld2", "sp1", "sp2", "lg0", "ld3", "co0", "lg1", "sm0",
-    "co1", "sp3", "lg2", "sm1", "co2", "gr0", "go0", "sm2", "tm0", "gr1", "lg3", "gr2", "m30", "m20", "go1",
-    "tm1", "co3", "m10", "go2", "r00", "m00", "r10", "sm3", "m31", "m21", "m11", "r11", "tm2", "gr3", "r01",
-    "m22", "m01", "go3", "tm3", "m32", "m12", "r02", "m23", "r12", "m02", "fi1", "m13", "m33", "r03", "r13",
-    "fi2", "m03", "fi0", "fi3",
+    "ga0", "ld0", "ga1", "sp0", "ld1", "ga2", "sp1", "lg0", "ld2", "ga3", "sp2", "co0", "sm0", "lg1", "ld3",
+    "co1", "sp3", "gr0", "sm1", "lg2", "go0", "co2", "tm0", "gr1", "lg3", "co3", "sm2", "m20", "go1", "tm1",
+    "sm3", "m30", "r00", "m10", "gr2", "m00", "go2", "m31", "r10", "tm2", "m21", "m11", "gr3", "m01", "r11",
+    "go3", "r01", "m32", "m12", "m22", "tm3", "m02", "r12", "r02", "m33", "m13", "m23", "fi0", "fi1", "m03",
+    "r03", "r13", "fi2", "fi3",
 )
 
 

time: 100 us -> 97.3 us (0.973); the launches traced: 100 us -> 96 us
  Pallas kernels: 96.5 us -> 92.4 us
    pallas_call x1, Pallas kernels: 96.5 us -> 92.4 us  [on_device(): pl.pallas_call(lambda *refs: kernel(SIZES, *refs), out_shape=(jax.ShapeDt...]
where the time goes in v4:
time: 97.3 us; the launch traced here: 96 us
  Pallas kernels  92.4 us (95%)
  local copies, waits for them, and re-layouts  2.93 us (3%)
    pallas_call x1, Pallas kernels, on_device(): pl.pallas_call(lambda *refs: kernel(SIZES, *refs), out_shape=(jax.ShapeDt...  92.4 us
    unnamed x2, local copies, waits for them, and re-layouts  2.93 us

profile of v4, /device:TPU:0, one launch (start us, length us, event | category | flops | bytes accessed | tf_op | source)
XLA Modules:
  0.0 96.0 jit_solution(4841071369954599760)
XLA Ops:
  0.6 92.4 %shard_map.68 = (bf16[192,896]{1,0:T(8,128)(2,1)}, f32[1,192]{1,0:T(1,128)}) custom-call(bf16[192,896]{1,0:T(8,128)(2,1)} %refs_0_.1, bf16[1792,1024]{1,0:T(8,128)(2,1)} %refs_1_.1, s32[1,192]{1,0:T(1,128)} %bitcast.5, s32[1,1024]{1,0:T(1,128)} %bitcast.4, f32[1,192]{1,0:T(1,128)} %bitcast.6), custom_call_target="tpu_custom_call" | custom-call | tf_op jit(solution)/shard_map/pallas_call | solution.py:462
  93.0 1.7 %copy.9 = bf16[192,896]{1,0:T(8,128)(2,1)} copy(bf16[192,896]{1,0:T(8,128)(2,1)} %get-tuple-element.8) | data formatting | bytes 688128
  94.8 1.2 %copy.10 = f32[192]{0:T(256)} copy(f32[192]{0:T(256)} %bitcast.7) | data formatting | bytes 1536

commit v5 on v4

--- a/solution.py
+++ b/solution.py
@@ -72,11 +72,11 @@
 
 
 PLAN = (
-    "ga0", "ld0", "ga1", "sp0", "ld1", "ga2", "sp1", "lg0", "ld2", "ga3", "sp2", "co0", "sm0", "lg1", "ld3",
-    "co1", "sp3", "gr0", "sm1", "lg2", "go0", "co2", "tm0", "gr1", "lg3", "co3", "sm2", "m20", "go1", "tm1",
-    "sm3", "m30", "r00", "m10", "gr2", "m00", "go2", "m31", "r10", "tm2", "m21", "m11", "gr3", "m01", "r11",
-    "go3", "r01", "m32", "m12", "m22", "tm3", "m02", "r12", "r02", "m33", "m13", "m23", "fi0", "fi1", "m03",
-    "r03", "r13", "fi2", "fi3",
+    "ga0", "ld0", "ga1", "sp0", "ld1", "ga2", "sp1", "ld2", "lg0", "ga3", "co0", "sp2", "sm0", "ld3", "lg1",
+    "co1", "sp3", "gr0", "sm1", "lg2", "go0", "co2", "tm0", "gr1", "lg3", "co3", "sm2", "go1", "m20", "tm1",
+    "m30", "m10", "sm3", "r00", "gr2", "r10", "m00", "m31", "m21", "go2", "tm2", "r11", "m11", "gr3", "go3",
+    "m01", "r01", "m32", "tm3", "m12", "m22", "r12", "fi1", "m23", "fi0", "m02", "m33", "r02", "m13", "m03",
+    "r03", "fi2", "r13", "fi3",
 )
 
 
@@ -498,6 +498,33 @@
                 collective_id=0, has_side_effects=True, vmem_limit_bytes=60 * 1024 * 1024
             ),
         )(hidden, head_weight, targets[None, :], vocab_mask[None, :], token_grad[None, :])
+        def hand_on(grad_ref, loss_ref, grad_out, loss_out, grad_buf, loss_buf, sem):
+            ins = [
+                pltpu.make_async_copy(loss_ref, loss_buf, sem.at[0]),
+                pltpu.make_async_copy(grad_ref, grad_buf, sem.at[1]),
+            ]
+            outs = [
+                pltpu.make_async_copy(loss_buf, loss_out, sem.at[2]),
+                pltpu.make_async_copy(grad_buf, grad_out, sem.at[3]),
+            ]
+            for copy in ins:
+                copy.start()
+            for copy, after in zip(ins, outs):
+                copy.wait()
+                after.start()
+            for copy in outs:
+                copy.wait()
+
+        hidden_grad, loss = pl.pallas_call(
+            hand_on,
+            out_shape=(
+                jax.ShapeDtypeStruct((rows, feats), BF),
+                jax.ShapeDtypeStruct((1, rows), F32),
+            ),
+            in_specs=[hbm, hbm],
+            out_specs=(hbm, hbm),
+            scratch_shapes=[pltpu.VMEM((rows, feats), BF), pltpu.VMEM((1, rows), F32), dma((4,))],
+        )(hidden_grad, loss)
         return (hidden_grad, loss.reshape(rows))
 
     return on_device

time: 97.3 us -> 93.3 us (0.959); the launches traced: 96 us -> 93.1 us
  local copies, waits for them, and re-layouts: 2.93 us -> 0 us
    unnamed x2 -> x0, local copies, waits for them, and re-layouts: 2.93 us -> none
    pallas_call x0 -> x1, Pallas kernels: none -> 1.75 us  [on_device(): pl.pallas_call(hand_on, out_shape=(jax.ShapeDtypeStruct((rows, feats), BF...]
    pallas_call x1, Pallas kernels: 92.4 us -> 90.7 us  [on_device(): pl.pallas_call(lambda *refs: kernel(SIZES, *refs), out_shape=(jax.ShapeDt...]
where the time goes in v5:
time: 93.3 us; the launch traced here: 93.1 us
  Pallas kernels  92.4 us (99%)
    pallas_call x1, Pallas kernels, on_device(): pl.pallas_call(lambda *refs: kernel(SIZES, *refs), out_shape=(jax.ShapeDt...  90.7 us

profile of v5, /device:TPU:0, one launch (start us, length us, event | category | flops | bytes accessed | tf_op | source)
XLA Modules:
  0.0 93.1 jit_solution(2886858162695921327)
XLA Ops:
  0.6 90.7 %shard_map.68 = (bf16[192,896]{1,0:T(8,128)(2,1)}, f32[1,192]{1,0:T(1,128)}) custom-call(bf16[192,896]{1,0:T(8,128)(2,1)} %refs_0_.1, bf16[1792,1024]{1,0:T(8,128)(2,1)} %refs_1_.1, s32[1,192]{1,0:T(1,128)} %bitcast.5, s32[1,1024]{1,0:T(1,128)} %bitcast.4, f32[1,192]{1,0:T(1,128)} %bitcast.6), custom_call_target="tpu_custom_call" | custom-call | tf_op jit(solution)/shard_map/pallas_call | solution.py:462
  91.3 1.7 %shard_map.69 = (bf16[192,896]{1,0:T(8,128)(2,1)}, f32[1,192]{1,0:T(1,128)}) custom-call(bf16[192,896]{1,0:T(8,128)(2,1)} %get-tuple-element.6.grad_ref, f32[1,192]{1,0:T(1,128)} %get-tuple-element.7.loss_ref), custom_call_target="tpu_custom_call" | custom-call | tf_op jit(solution)/shard_map/pallas_call | solution.py:518

commit v6 on v5

--- a/solution.py
+++ b/solution.py
@@ -73,10 +73,10 @@
 
 PLAN = (
     "ga0", "ld0", "ga1", "sp0", "ld1", "ga2", "sp1", "ld2", "lg0", "ga3", "co0", "sp2", "sm0", "ld3", "lg1",
-    "co1", "sp3", "gr0", "sm1", "lg2", "go0", "co2", "tm0", "gr1", "lg3", "co3", "sm2", "go1", "m20", "tm1",
-    "m30", "m10", "sm3", "r00", "gr2", "r10", "m00", "m31", "m21", "go2", "tm2", "r11", "m11", "gr3", "go3",
-    "m01", "r01", "m32", "tm3", "m12", "m22", "r12", "fi1", "m23", "fi0", "m02", "m33", "r02", "m13", "m03",
-    "r03", "fi2", "r13", "fi3",
+    "co1", "sp3", "gr0", "lg2", "sm1", "co2", "go0", "tm0", "gr1", "lg3", "m20", "sm2", "go1", "co3", "m30",
+    "r00", "tm1", "m10", "gr2", "sm3", "r10", "m21", "go2", "m00", "m31", "tm2", "m11", "r01", "gr3", "m01",
+    "m22", "r11", "m32", "go3", "r02", "fi0", "tm3", "m12", "r12", "m23", "m02", "m33", "m13", "m03", "r03",
+    "r13", "fi2", "fi1", "fi3",
 )
 
 
@@ -227,7 +227,7 @@
     def relay_copy(g, cc):
         return rcopy(tin.at[cc, span(g)], fin.at[z, span(g)], r_send.at[g, cc], f_recv.at[g, z], ((1 - y) * 2 + cc) * 2 + x, me_t)
 
-    tile = 256
+    tile = 512
 
     def passed(g):
         @pl.when(is_inner)

time: 93.3 us -> 92.4 us (level)
  no operation moved by 1% of the time
where the time goes in v6:
time: 92.4 us; the launch traced here: 92.2 us
  Pallas kernels  91.6 us (99%)
    pallas_call x1, Pallas kernels, on_device(): pl.pallas_call(lambda *refs: kernel(SIZES, *refs), out_shape=(jax.ShapeDt...  89.8 us

profile of v6, /device:TPU:0, one launch (start us, length us, event | category | flops | bytes accessed | tf_op | source)
XLA Modules:
  0.0 92.2 jit_solution(14765171709386399843)
XLA Ops:
  0.6 89.8 %shard_map.68 = (bf16[192,896]{1,0:T(8,128)(2,1)}, f32[1,192]{1,0:T(1,128)}) custom-call(bf16[192,896]{1,0:T(8,128)(2,1)} %refs_0_.1, bf16[1792,1024]{1,0:T(8,128)(2,1)} %refs_1_.1, s32[1,192]{1,0:T(1,128)} %bitcast.5, s32[1,1024]{1,0:T(1,128)} %bitcast.4, f32[1,192]{1,0:T(1,128)} %bitcast.6), custom_call_target="tpu_custom_call" | custom-call | tf_op jit(solution)/shard_map/pallas_call | solution.py:462
  90.4 1.7 %shard_map.69 = (bf16[192,896]{1,0:T(8,128)(2,1)}, f32[1,192]{1,0:T(1,128)}) custom-call(bf16[192,896]{1,0:T(8,128)(2,1)} %get-tuple-element.6.grad_ref, f32[1,192]{1,0:T(1,128)} %get-tuple-element.7.loss_ref), custom_call_target="tpu_custom_call" | custom-call | tf_op jit(solution)/shard_map/pallas_call | solution.py:518

commit v7 on v6

--- a/solution.py
+++ b/solution.py
@@ -84,7 +84,7 @@
     sizes,
     hidden_ref, weight_ref, targets_ref, mask_ref, grad_ref,
     out_ref, loss_ref,
-    hid, wbuf, land, hb, plog, pin, xo, xi, msk, stats_out, stats_in, loss_rows, dl,
+    out_buf, loss_buf, o_sem, hid, wbuf, land, hb, plog, pin, xo, xi, msk, stats_out, stats_in, loss_rows, dl,
     mix_out, mix_in, near, eo, tin, fin,
     l_sem, w_sem, a_send, a_recv, n_recv, n_send, x_send, x_recv, p_send, p_recv, c_send, c_recv,
     s_send, s_recv, d_send, d_recv, m_send, m_recv, e_send, f_recv, t_recv, r_send,
@@ -388,6 +388,11 @@
             rcopy(eo.at[0, span(g)], tin.at[cc, span(g)], e_send.at[g, 0], t_recv.at[g, cc], me_v, (1 - y) * 2 + cc).wait_recv()
             relay_copy(g, cc).start()
 
+    def out_copy(g):
+        return pltpu.make_async_copy(out_buf.at[span(g)], out_ref.at[span(g)], o_sem.at[g])
+
+    loss_copy = pltpu.make_async_copy(loss_buf, loss_ref, o_sem.at[groups])
+
     def finish(g):
         total = None
         for zz in range(4):
@@ -397,7 +402,8 @@
         for zz in range(4):
             term = fin[zz, span(g), :].astype(F32)
             total = term if total is None else total + term
-        out_ref[span(g), :] = total.astype(BF)
+        out_buf[span(g), :] = total.astype(BF)
+        out_copy(g).start()
 
     steps = {
         "ga": gather, "ld": passed, "sp": spread, "lg": logits_of, "co": cross_over, "sm": softmax_of, "gr": grads_of, "go": grads_on,
@@ -407,10 +413,14 @@
         steps[f"m{r}"] = lambda g, r=r: mixed(g, r)
     for r in range(2):
         steps[f"r{r}"] = lambda g, r=r: relayed(g, r)
+    pending = set(range(groups))
     for item in PLAN:
         steps[item[:2]](int(item[2:]))
-
-    loss_ref[...] = jnp.concatenate([loss_rows[g][:, 0:sizes[g]] for g in range(groups)], axis=1)
+        if item[:2] == "gr":
+            pending.remove(int(item[2:]))
+            if not pending:
+                loss_buf[...] = jnp.concatenate([loss_rows[g][:, 0:sizes[g]] for g in range(groups)], axis=1)
+                loss_copy.start()
 
     for g in range(groups):
         a_copy(g).wait_send()
@@ -449,6 +459,8 @@
             stat_copy(g, k).wait_send()
         for i in range(3):
             grad_copy(g, i).wait_send()
+        out_copy(g).wait()
+    loss_copy.wait()
 
 
 def fused(vocab_size, tok_size):
@@ -466,8 +478,11 @@
                 jax.ShapeDtypeStruct((1, rows), F32),
             ),
             in_specs=[hbm, hbm] + [vmem] * 3,
-            out_specs=(vmem, vmem),
+            out_specs=(hbm, hbm),
             scratch_shapes=[
+                pltpu.VMEM((rows, feats), BF),
+                pltpu.VMEM((1, rows), F32),
+                dma((groups + 1,)),
                 pltpu.VMEM((rows, feats), BF),
                 pltpu.VMEM((2 * feats, width), BF),
                 pltpu.VMEM((2, rows, feats), BF),

time: 92.4 us -> 92.2 us (level)
  no operation moved by 1% of the time
where the time goes in v7:
time: 92.2 us; the launch traced here: 92 us
  Pallas kernels  91.3 us (99%)
    pallas_call x1, Pallas kernels, on_device(): pl.pallas_call(lambda *refs: kernel(SIZES, *refs), out_shape=(jax.ShapeDt...  89.6 us

profile of v7, /device:TPU:0, one launch (start us, length us, event | category | flops | bytes accessed | tf_op | source)
XLA Modules:
  0.0 92.0 jit_solution(513892697596396141)
XLA Ops:
  0.6 89.6 %shard_map.68 = (bf16[192,896]{1,0:T(8,128)(2,1)}, f32[1,192]{1,0:T(1,128)}) custom-call(bf16[192,896]{1,0:T(8,128)(2,1)} %refs_0_.1, bf16[1792,1024]{1,0:T(8,128)(2,1)} %refs_1_.1, s32[1,192]{1,0:T(1,128)} %bitcast.5, s32[1,1024]{1,0:T(1,128)} %bitcast.4, f32[1,192]{1,0:T(1,128)} %bitcast.6), custom_call_target="tpu_custom_call" | custom-call | tf_op jit(solution)/shard_map/pallas_call | solution.py:474
  90.2 1.7 %shard_map.69 = (bf16[192,896]{1,0:T(8,128)(2,1)}, f32[1,192]{1,0:T(1,128)}) custom-call(bf16[192,896]{1,0:T(8,128)(2,1)} %get-tuple-element.6.grad_ref, f32[1,192]{1,0:T(1,128)} %get-tuple-element.7.loss_ref), custom_call_target="tpu_custom_call" | custom-call | tf_op jit(solution)/shard_map/pallas_call | solution.py:533
